TPU v7x, 32 devices: a whole 2x2x4 slice. The times are simulated.
32 devices in a mesh: groups: 2 (over x), seq: 8 (over z, y), dec: 2 (over core).
Axes of the slice: x: 2, y: 2, z: 4, core: 2. Of those that a mesh axis runs over, the one named last changes fastest.
Arguments:
- tokens: bfloat16 [2048, 4096], P(('groups', 'seq')), parts along dimension 0, may hold values from -64 to 64
- norm_gain: float32 [4096], replicated, may hold values from 0.25 to 1.75
- w_query: bfloat16 [4096, 2048], P('seq', 'dec'), may hold values from -0.140625 to 0.140625
- w_key: bfloat16 [4096, 512], P('seq', 'dec'), may hold values from -0.140625 to 0.140625
- w_value: bfloat16 [4096, 512], P('seq', 'dec'), may hold values from -0.09375 to 0.09375
- block_order: int32 [32], P('groups'), parts along dimension 0, may hold values from 0 to 15, as said below
- block_docs: int32 [32], P('groups'), parts along dimension 0, may hold values from 0 to 3, never falling along the last dimension, each value on 1 to 8 neighbouring positions
- head_owner: int32 [8], P('groups'), parts along dimension 0, may hold values from 0 to 3, as said below
- prev_kv: bfloat16 [2048, 2, 4, 128], P(('groups', 'seq', 'dec')), parts along dimension 0, may hold values from -6 to 6
Outputs:
- attended: bfloat16 [2048, 2048], P(('groups', 'seq'), 'dec'), parts along dimension 0
- decode_cache: bfloat16 [2048, 2, 4, 128], P(('groups', 'seq'), None, 'dec'), parts along dimension 0
There are 2 independent parts, one for each index of `groups`. A program takes and returns all parts, laid end to end along the dimension named above; an argument that names none is the same for every part. Nothing has to cross between parts.
Inputs may be any that keep to these rules, and one draw needn't show every extreme that they name: `block_order`: cycle slots 2i and 2i + 1 hold the blocks b and 15 - b for some b; every block stands in exactly one slot. `head_owner`: each key-value head stands in exactly one decode slot.
All inputs are finite; a program needn't handle non-finite values.
Results may differ from a plain program's by a relative error of at most 0.0035.
The roundings to bfloat16 on the way count: a program that leaves them out, or rounds other values in their place, can miss the bound.
Values may be sent and summed in bfloat16 or wider, within the bound.
A program may use at most 64 MiB of HBM per device.

v0:
```python
import math
import jax
import jax.numpy as jnp
from jax import lax
from jax.sharding import PartitionSpec as P

HD = 128


def rotate(values, positions):
    half_width = values.shape[-1] // 2
    frequency = 500000.0 ** (-jnp.arange(half_width, dtype=jnp.float32) / half_width)
    angles = positions[:, None].astype(jnp.float32) * frequency[None, :]
    cosines = jnp.cos(angles)[:, None, :]
    sine_terms = jnp.sin(angles)[:, None, :]
    lower_half = values[..., :half_width]
    upper_half = values[..., half_width:]
    return jnp.concatenate(
        [
            lower_half * cosines - upper_half * sine_terms,
            upper_half * cosines + lower_half * sine_terms,
        ],
        -1,
    )


def per_device(
    tokens, norm_gain, w_query, w_key, w_value, block_order, block_docs, head_owner, prev_kv
):
    rows_dev = tokens.shape[0]
    block_rows = rows_dev // 2
    inputs = tokens.astype(jnp.float32)
    normed = (
        inputs * lax.rsqrt(jnp.mean(inputs * inputs, -1, keepdims=True) + 1e-05) * norm_gain
    ).astype(jnp.bfloat16)

    def add_piece(piece):
        return jnp.dot(normed, piece, preferred_element_type=jnp.float32)

    pieces = (
        lax.all_gather(w_query, "seq", axis=0, tiled=True),
        lax.all_gather(w_key, "seq", axis=0, tiled=True),
        lax.all_gather(w_value, "seq", axis=0, tiled=True),
    )
    query_full, key_full, value_full = tuple((add_piece(piece) for piece in pieces))
    total_rows = rows_dev * lax.axis_size("seq")
    row_ids = jnp.arange(total_rows, dtype=jnp.int32)
    natural = jnp.take(block_order, row_ids // block_rows)
    pos_all = natural * block_rows + row_ids % block_rows
    doc_all = jnp.take(block_docs, natural)
    offset = lax.axis_index("seq") * rows_dev
    my_pos = lax.dynamic_slice_in_dim(pos_all, offset, rows_dev)
    my_doc = lax.dynamic_slice_in_dim(doc_all, offset, rows_dev)
    local_kv = key_full.shape[1] // HD
    local_heads = query_full.shape[1] // HD
    group_size = local_heads // local_kv
    queries = rotate(query_full.reshape(rows_dev, local_heads, HD), my_pos).astype(jnp.bfloat16)
    query_groups = queries.reshape(rows_dev, local_kv, group_size, HD).transpose(1, 2, 0, 3)
    key_rows = (
        rotate(key_full.reshape(rows_dev, local_kv, HD), my_pos)
        .astype(jnp.bfloat16)
        .reshape(rows_dev, local_kv * HD)
    )
    value_rows = value_full.astype(jnp.bfloat16)
    scale = 1.0 / math.sqrt(HD)
    start_max = jnp.full((local_kv, group_size, rows_dev, 1), -jnp.inf, jnp.float32)
    start_sum = jnp.zeros((local_kv, group_size, rows_dev, 1), jnp.float32)
    start_weighted = jnp.zeros((local_kv, group_size, rows_dev, HD), jnp.float32)
    key_piece = lax.all_gather(key_rows, "seq", axis=0, tiled=True)
    value_piece = lax.all_gather(value_rows, "seq", axis=0, tiled=True)
    count = key_piece.shape[0]
    allowed = (pos_all[None, :] <= my_pos[:, None]) & (doc_all[None, :] == my_doc[:, None])

    def update(state):
        running_max, running_sum, weighted = state
        scores = (
            jnp.einsum(
                "ghtd,sgd->ghts",
                query_groups,
                key_piece.reshape(count, local_kv, HD),
                preferred_element_type=jnp.float32,
            )
            * scale
        )
        scores = jnp.where(allowed, scores, -jnp.inf)
        new_max = jnp.max(scores, -1, keepdims=True)
        shift_by = jnp.where(new_max == -jnp.inf, 0.0, new_max)
        weights = jnp.exp(scores - shift_by)
        rescale = jnp.exp(running_max - shift_by)
        running_sum = running_sum * rescale + jnp.sum(weights, -1, keepdims=True)
        weighted = weighted * rescale + jnp.einsum(
            "ghts,sgd->ghtd",
            weights.astype(jnp.bfloat16),
            value_piece.reshape(count, local_kv, HD),
            preferred_element_type=jnp.float32,
        )
        return (new_max, running_sum, weighted)

    final_max, final_sum, final_weighted = lax.cond(
        jnp.any(allowed), update, lambda state: state, (start_max, start_sum, start_weighted)
    )
    attended = (
        (final_weighted / final_sum)
        .transpose(2, 0, 1, 3)
        .reshape(rows_dev, local_heads * HD)
        .astype(jnp.bfloat16)
    )
    head_count = prev_kv.shape[2]
    selector = (head_owner[:, None] == jnp.arange(head_count, dtype=jnp.int32)[None, :]).astype(
        jnp.bfloat16
    )
    ordered = jnp.einsum(
        "tcjd,sj->tcsd", prev_kv, selector, preferred_element_type=jnp.float32
    ).astype(jnp.bfloat16)
    decode_cache = lax.all_to_all(ordered, "dec", split_axis=2, concat_axis=0, tiled=True)
    return (attended, decode_cache)


def solution(mesh):
    in_specs = (
        P(("groups", "seq"), None),
        P(),
        P("seq", "dec"),
        P("seq", "dec"),
        P("seq", "dec"),
        P("groups"),
        P("groups"),
        P("groups"),
        P(("groups", "seq", "dec"), None, None, None),
    )
    out_specs = (P(("groups", "seq"), "dec"), P(("groups", "seq"), None, "dec", None))
    return jax.shard_map(
        per_device, mesh=mesh, in_specs=in_specs, out_specs=out_specs, check_vma=False
    )
```

profile of v0, /device:TPU:0, one launch (start us, length us, event | category | flops | bytes accessed | tf_op | source)
XLA Modules:
  0.0 262.9 jit_solution(15112407311073166945)
XLA Ops:
  8.0 0.7 all-gather.8.cloned.1.call-update
  9.4 1.0 fusion.21
  10.4 0.8 copy.22
  11.2 3.4 %all-to-all-start = ((bf16[64,2,4,128]{3,1,0,2:T(2,128)(2,1)}), bf16[64,2,4,128]{3,1,0,2:T(2,128)(2,1)S(1)}, u32[]{:S(2)}, u32[]{:S(2)}) async-start(bf16[64,2,4,128]{3,1,0,2:T(2,128)(2,1)} %copy.22), calls=%async_computation | async-start | bytes 262144 | tf_op jit(solution)/shard_map/all_to_all | solution.py:115
  14.6 2.0 fusion.58
  16.6 1.9 fusion.59
  18.5 19.9 %select_select_fusion = s32[1024]{0:T(1024)S(1)} fusion(s32[]{:T(128)} %bitcast.35, s32[]{:T(128)} %bitcast.34, s32[]{:T(128)} %bitcast.33, s32[]{:T(128)} %bitcast.32, s32[]{:T(128)} %bitcast.31, s32[]{:T(128)} %bitcast.30, s32[]{:T(128)} %bitcast.29, s32[]{:T(128)} %bitcast.28, s32[]{:T(128)} %bitcast.27, s32[]{:T(128)} %bitcast.26, s32[]{:T(128)} %bitcast.25, ...), kind=kLoop, calls=%fused_computation.72 | loop fusion | flops 83968 | bytes 4224 | tf_op jit(solution)/shard_map/jit(_take)/select_n | solution.py:50
  38.5 10.0 %fusion.29 = s32[1024]{0:T(1024)S(1)} fusion(s32[]{:T(128)} %bitcast.19, s32[]{:T(128)} %bitcast.18, s32[]{:T(128)} %bitcast.17, s32[]{:T(128)} %bitcast.16, s32[]{:T(128)} %bitcast.15, s32[]{:T(128)} %bitcast.14, s32[]{:T(128)} %bitcast.13, s32[]{:T(128)} %bitcast.12, s32[]{:T(128)} %bitcast.11, s32[]{:T(128)} %bitcast.10, s32[]{:T(128)} %bitcast.9, ...), kind=kLoop, calls=%fused_computation.53 | loop fusion | flops 52224 | bytes 4160 | tf_op jit(solution)/shard_map/add | solution.py:49
  48.6 0.8 fusion.57
  50.1 0.9 copy.23
  50.9 1.5 fusion.18
  52.8 9.2 %all-gather.4.cloned.1.call-done = bf16[4096,256]{1,0:T(8,128)(2,1)} async-done(((bf16[512,256]{1,0:T(8,128)(2,1)}), bf16[4096,256]{1,0:T(8,128)(2,1)}) %all-gather.4.cloned.1.call-update) | async-done | bytes 2097168 | tf_op jit(solution)/shard_map/all_gather | solution.py:42
  62.0 2.4 fusion.54
  65.0 32.8 %all_gather.16 = bf16[1024,256]{1,0:T(8,128)(2,1)S(1)} all-gather(bf16[128,256]{1,0:T(8,128)(2,1)S(1)} %bitcast.75), channel_id=1, replica_groups=mesh['groups'=2,'seq'=8,'dec'=2] {'seq'}, dimensions={0}, use_global_device_ids=true | all-gather | bytes 589824 | tf_op jit(solution)/shard_map/all_gather | solution.py:69
  97.8 15.3 %all-gather.8.cloned.1.call-done = bf16[4096,256]{1,0:T(8,128)(2,1)} async-done(((bf16[512,256]{1,0:T(8,128)(2,1)}), bf16[4096,256]{1,0:T(8,128)(2,1)}) %all-gather.8.cloned.1.call-update) | async-done | bytes 2097168 | tf_op jit(solution)/shard_map/all_gather | solution.py:43
  113.1 2.1 convolution_convert_fusion.1
  115.2 33.3 %all_gather.19 = bf16[1024,256]{1,0:T(8,128)(2,1)S(1)} all-gather(bf16[128,256]{1,0:T(8,128)(2,1)S(1)} %convolution_convert_fusion.1), channel_id=1, replica_groups=mesh['groups'=2,'seq'=8,'dec'=2] {'seq'}, dimensions={0}, use_global_device_ids=true | all-gather | bytes 589824 | tf_op jit(solution)/shard_map/all_gather | solution.py:70
  148.5 93.5 %all-gather.6.cloned.1.call-done = bf16[4096,1024]{1,0:T(8,128)(2,1)} async-done(((bf16[512,1024]{1,0:T(8,128)(2,1)}), bf16[4096,1024]{1,0:T(8,128)(2,1)}) %all-gather.6.cloned.1.call-update) | async-done | bytes 8388624 | tf_op jit(solution)/shard_map/all_gather | solution.py:41
  242.0 4.7 %convolution_bitcast_fusion = f32[16,8,8,128]{3,1,2,0:T(8,128)S(1)} fusion(bf16[4096,1024]{1,0:T(8,128)(2,1)} %all-gather.6.cloned.1.call-done, bf16[128,4096]{1,0:T(8,128)(2,1)S(1)} %copy-done.2, f32[4096]{0:T(1024)S(1)} %copy-done.3, f32[128]{0:T(128)S(1)} %add_rsqrt_fusion), kind=kOutput, calls=%fused_computation.25 | convolution fusion | flops 1075838976 | bytes 9978368 | tf_op jit(solution)/shard_map/dot_general | solution.py:38
  247.3 7.8 %conditional.1 = (f32[2,4,128,1]{2,1,0,3:T(4,128)S(1)}, f32[2,4,128,128]{3,2,1,0:T(8,128)S(1)}) conditional(s32[]{:T(128)} %convert_element_type.43, () %tuple.17, (pred[128,1024]{1,0:T(8,128)(4,1)S(1)}, bf16[1024,256]{1,0:T(8,128)(2,1)S(1)}, bf16[2,4,128,128]{3,2,1,0:T(8,128)(2,1)S(1)}, bf16[1024,256]{1,0:T(8,128)(2,1)S(1)}) %tuple.18), branch_computations={%region_2.4_spmd, %region_3.7_spmd} | conditional | flops 548543488 | bytes 33730604 | solution.py:99
  247.4 2.8 %fusion = (f32[2,4,128]{2,1,0:T(4,128)S(1)}, f32[2,4,128,1024]{3,2,1,0:T(8,128)}) fusion(pred[128,1024]{1,0:T(8,128)(4,1)S(1)} %get-tuple-element.3, bf16[2,4,128,128]{3,2,1,0:T(8,128)(2,1)S(1)} %get-tuple-element.10, bf16[1024,2,128,1]{2,1,0,3:T(2,128)(2,1)S(1)} %bitcast.69), kind=kOutput, calls=%fused_computation.2 | convolution fusion | flops 271580160 | bytes 5115904 | tf_op jit(solution)/shard_map/cond/branch_1_fun/ghtd,sgd->ghts/dot_general | solution.py:77
  250.4 3.5 %fusion.6 = f32[2,4,128,128]{3,2,1,0:T(8,128)S(1)} fusion(f32[2,4,128,1024]{3,2,1,0:T(8,128)} %get-tuple-element.26, f32[2,4,128]{2,1,0:T(4,128)S(1)} %get-tuple-element.24, pred[128,1024]{1,0:T(8,128)(4,1)S(1)} %get-tuple-element.3, bf16[1024,2,128,1]{2,1,0,3:T(2,128)(2,1)S(1)} %bitcast.72, f32[2,4,128]{2,1,0:T(4,128)S(1)} %get-tuple-element.23), kind=kOutput, calls=%fused_computation.7 | convolution fusion | flops 272760832 | bytes 5382144 | tf_op jit(solution)/shard_map/cond/branch_1_fun/ghts,sgd->ghtd/dot_general | solution.py:91
  253.9 1.1 fusion.2
  255.5 0.9 convert_element_type.51
  (34 shorter events, 3.8 us)
Async XLA Ops:
  7.2 2.2 copy-start
  7.2 54.9 %all-gather.4.cloned.1.call-start = ((), (), s32[]{:S(2)}) async-start(), calls=%async_computation.1 | async-start | bytes 2359296 | tf_op jit(solution)/shard_map/all_gather | solution.py:42
  7.9 105.2 %all-gather.8.cloned.1.call-start = ((), (), s32[]{:S(2)}) async-start(), calls=%async_computation.3 | async-start | bytes 2359296 | tf_op jit(solution)/shard_map/all_gather | solution.py:43
  8.7 233.3 %all-gather.6.cloned.1.call-start = ((), (), s32[]{:S(2)}) async-start(), calls=%async_computation.2 | async-start | bytes 9437184 | tf_op jit(solution)/shard_map/all_gather | solution.py:41
  9.4 103.7 %copy-start.2 = (bf16[128,4096]{1,0:T(8,128)(2,1)S(1)}, bf16[128,4096]{1,0:T(8,128)(2,1)}, u32[]{:S(2)}) copy-start(bf16[128,4096]{1,0:T(8,128)(2,1)} %param.13) | copy-start | bytes 3145732
  9.4 103.7 %copy-start.3 = (f32[4096]{0:T(1024)S(1)}, f32[4096]{0:T(1024)}, u32[]{:S(2)}) copy-start(f32[4096]{0:T(1024)} %param.14) | copy-start | bytes 49156
  11.2 38.8 %all-to-all-start = ((bf16[64,2,4,128]{3,1,0,2:T(2,128)(2,1)}), bf16[64,2,4,128]{3,1,0,2:T(2,128)(2,1)S(1)}, u32[]{:S(2)}, u32[]{:S(2)}) async-start(bf16[64,2,4,128]{3,1,0,2:T(2,128)(2,1)} %copy.22), calls=%async_computation | async-start | bytes 262144 | tf_op jit(solution)/shard_map/all_to_all | solution.py:115
  250.4 3.6 %copy-start.1 = (f32[2,4,128,1024]{3,2,1,0:T(8,128)S(1)}, f32[2,4,128,1024]{3,2,1,0:T(8,128)}, u32[]{:S(2)}) copy-start(f32[2,4,128,1024]{3,2,1,0:T(8,128)} %get-tuple-element.26) | copy-start | bytes 12582916 | tf_op jit(solution)/shard_map/cond
Sparse Core Ops, SparseCore 0:
  10.1 51.8 all-gather.3
  64.2 48.8 all-gather.7
  115.2 126.7 all-gather.5
where the time goes:
time: 264 us; the launch traced here: 263 us
  waiting for transfers between devices  120 us (45%)
  blocking collectives  66.1 us (25%)
  other arithmetic  34.9 us (13%)
  matrix products  16.5 us (6%)
  between operations  14.6 us (6%)
  local copies, waits for them, and re-layouts  7.21 us (3%)
  starting transfers between devices  3.49 us (1%)
    all_gather x1, waiting for transfers between devices, per_device(): lax.all_gather(w_query, 'seq', axis=0, tiled=True)  93.5 us
    all_gather x1, blocking collectives, per_device(): value_piece = lax.all_gather(value_rows, 'seq', axis=0, tiled=True)  33.3 us
    all_gather x1, blocking collectives, per_device(): key_piece = lax.all_gather(key_rows, 'seq', axis=0, tiled=True)  32.8 us
    select_n x1, other arithmetic, per_device(): doc_all = jnp.take(block_docs, natural)  19.9 us
    all_gather x1, waiting for transfers between devices, per_device(): lax.all_gather(w_value, 'seq', axis=0, tiled=True)  15.3 us
    add x1, other arithmetic, per_device(): pos_all = natural * block_rows + row_ids % block_rows  9.98 us
    all_gather x1, waiting for transfers between devices, per_device(): lax.all_gather(w_key, 'seq', axis=0, tiled=True)  9.24 us
    dot_general x3, matrix products, add_piece(): return jnp.dot(normed, piece, preferred_element_type=jnp.float32)  9.16 us
  transfers between devices with their start and end apart: 4, of which 3 were waited for; matrix products, arithmetic and copies ran while one was open for 17% of the time, Pallas kernels for 0%

commit v1 on v0

--- a/solution.py
+++ b/solution.py
@@ -66,7 +66,12 @@
     start_max = jnp.full((local_kv, group_size, rows_dev, 1), -jnp.inf, jnp.float32)
     start_sum = jnp.zeros((local_kv, group_size, rows_dev, 1), jnp.float32)
     start_weighted = jnp.zeros((local_kv, group_size, rows_dev, HD), jnp.float32)
-    key_piece = lax.all_gather(key_rows, "seq", axis=0, tiled=True)
+    ring = [key_rows]
+    for hop in range(7):
+        ring.append(lax.ppermute(ring[-1], "seq", [(dev, (dev + 1) % 8) for dev in range(8)]))
+    key_piece = jnp.roll(
+        jnp.concatenate(ring[::-1], axis=0), (lax.axis_index("seq") + 1) * ring[0].shape[0], axis=0
+    )
     value_piece = lax.all_gather(value_rows, "seq", axis=0, tiled=True)
     count = key_piece.shape[0]
     allowed = (pos_all[None, :] <= my_pos[:, None]) & (doc_all[None, :] == my_doc[:, None])

time: 264 us -> 266 us (level)
  waiting for transfers between devices: 120 us -> 154 us
  blocking collectives: 66.1 us -> 34.9 us
    all_gather x1 -> x0, blocking collectives: 32.8 us -> none  [per_device(): key_piece = lax.all_gather(key_rows, 'seq', axis=0, tiled=True)]
    all_gather x1, waiting for transfers between devices: 9.24 us -> 38.8 us  [per_device(): lax.all_gather(w_key, 'seq', axis=0, tiled=True)]
    ppermute x0 -> x7, waiting for transfers between devices: none -> 26.5 us  [per_device(): lax.ppermute(ring[-1], 'seq', [(dev, (dev + 1) % 8) for dev in range(8)])]
    all_gather x1, waiting for transfers between devices: 15.3 us -> 0.01 us  [per_device(): lax.all_gather(w_value, 'seq', axis=0, tiled=True)]
    all_gather x1, waiting for transfers between devices: 93.5 us -> 86.7 us  [per_device(): lax.all_gather(w_query, 'seq', axis=0, tiled=True)]
  transfers between devices with their start and end apart: 4 -> 11, of which waited for: 3 -> 7; matrix products, arithmetic and copies ran while one was open for 17% -> 16% of each run, Pallas kernels for 0% -> 0%
where the time goes in v1:
time: 266 us; the launch traced here: 265 us
  waiting for transfers between devices  154 us (58%)
  blocking collectives  34.9 us (13%)
  other arithmetic  34.5 us (13%)
  matrix products  15.9 us (6%)
  between operations  14.7 us (6%)
  local copies, waits for them, and re-layouts  6.49 us (2%)
  starting transfers between devices  4.12 us (2%)
    all_gather x1, waiting for transfers between devices, per_device(): lax.all_gather(w_query, 'seq', axis=0, tiled=True)  86.7 us
    all_gather x1, waiting for transfers between devices, per_device(): lax.all_gather(w_key, 'seq', axis=0, tiled=True)  38.8 us
    all_gather x1, blocking collectives, per_device(): value_piece = lax.all_gather(value_rows, 'seq', axis=0, tiled=True)  34.9 us
    ppermute x7, waiting for transfers between devices, per_device(): lax.ppermute(ring[-1], 'seq', [(dev, (dev + 1) % 8) for dev in range(8)])  26.5 us
    select_n x1, other arithmetic, per_device(): doc_all = jnp.take(block_docs, natural)  19.7 us
    add x1, other arithmetic, per_device(): pos_all = natural * block_rows + row_ids % block_rows  9.9 us
    dot_general x3, matrix products, add_piece(): return jnp.dot(normed, piece, preferred_element_type=jnp.float32)  9.18 us
  transfers between devices with their start and end apart: 11, of which 7 were waited for; matrix products, arithmetic and copies ran while one was open for 16% of the time, Pallas kernels for 0%

profile of v1, /device:TPU:0, one launch (start us, length us, event | category | flops | bytes accessed | tf_op | source)
XLA Modules:
  0.0 264.9 jit_solution(7781226547105861549)
XLA Ops:
  9.5 2.0 fusion.56
  11.4 9.9 %fusion.27 = s32[1024]{0:T(1024)S(1)} fusion(s32[]{:T(128)} %bitcast.15, s32[]{:T(128)} %bitcast.14, s32[]{:T(128)} %bitcast.13, s32[]{:T(128)} %bitcast.12, s32[]{:T(128)} %bitcast.11, s32[]{:T(128)} %bitcast.10, s32[]{:T(128)} %bitcast.9, s32[]{:T(128)} %bitcast.8, s32[]{:T(128)} %bitcast.7, s32[]{:T(128)} %bitcast.6, s32[]{:T(128)} %bitcast.5, ...), kind=kLoop, calls=%fused_computation.67 | loop fusion | flops 52224 | bytes 4160 | tf_op jit(solution)/shard_map/add | solution.py:49
  21.4 1.5 fusion.16
  23.3 38.8 %all-gather.4.cloned.1.call-done = bf16[4096,256]{1,0:T(8,128)(2,1)} async-done(((bf16[512,256]{1,0:T(8,128)(2,1)}), bf16[4096,256]{1,0:T(8,128)(2,1)}) %all-gather.4.cloned.1.call-update) | async-done | bytes 2097168 | tf_op jit(solution)/shard_map/all_gather | solution.py:42
  62.0 2.4 fusion.52
  65.8 6.4 %collective-permute-done = bf16[128,256]{0,1:T(8,128)(2,1)S(1)} collective-permute-done((bf16[128,256]{0,1:T(8,128)(2,1)S(1)}, bf16[128,256]{0,1:T(8,128)(2,1)S(1)}, u32[]{:S(2)}, u32[]{:S(2)}) %collective-permute-start) | collective-permute-done | bytes 65568 | tf_op jit(solution)/shard_map/ppermute | solution.py:71
  72.5 0.8 copy.32
  73.2 3.4 %all-to-all-start = ((bf16[64,2,4,128]{3,1,0,2:T(2,128)(2,1)}), bf16[64,2,4,128]{3,1,0,2:T(2,128)(2,1)S(1)}, u32[]{:S(2)}, u32[]{:S(2)}) async-start(bf16[64,2,4,128]{3,1,0,2:T(2,128)(2,1)} %copy.32), calls=%async_computation | async-start | bytes 262144 | tf_op jit(solution)/shard_map/all_to_all | solution.py:120
  76.6 4.1 %collective-permute-done.1 = bf16[128,256]{0,1:T(8,128)(2,1)S(1)} collective-permute-done((bf16[128,256]{0,1:T(8,128)(2,1)S(1)}, bf16[128,256]{0,1:T(8,128)(2,1)S(1)}, u32[]{:S(2)}, u32[]{:S(2)}) %collective-permute-start.1) | collective-permute-done | bytes 65568 | tf_op jit(solution)/shard_map/ppermute | solution.py:71
  81.4 6.3 %collective-permute-done.2 = bf16[128,256]{0,1:T(8,128)(2,1)S(1)} collective-permute-done((bf16[128,256]{0,1:T(8,128)(2,1)S(1)}, bf16[128,256]{0,1:T(8,128)(2,1)S(1)}, u32[]{:S(2)}, u32[]{:S(2)}) %collective-permute-start.2) | collective-permute-done | bytes 65568 | tf_op jit(solution)/shard_map/ppermute | solution.py:71
  87.6 19.7 %select_select_fusion = s32[1024]{0:T(1024)S(1)} fusion(s32[]{:T(128)} %bitcast.31, s32[]{:T(128)} %bitcast.30, s32[]{:T(128)} %bitcast.29, s32[]{:T(128)} %bitcast.28, s32[]{:T(128)} %bitcast.27, s32[]{:T(128)} %bitcast.26, s32[]{:T(128)} %bitcast.25, s32[]{:T(128)} %bitcast.24, s32[]{:T(128)} %bitcast.23, s32[]{:T(128)} %bitcast.22, s32[]{:T(128)} %bitcast.21, ...), kind=kLoop, calls=%fused_computation.86 | loop fusion | flops 83968 | bytes 4224 | tf_op jit(solution)/shard_map/jit(_take)/select_n | solution.py:50
  107.5 1.0 fusion.55
  109.1 0.9 copy.33
  110.0 4.9 %collective-permute-done.4 = bf16[128,256]{0,1:T(8,128)(2,1)S(1)} collective-permute-done((bf16[128,256]{0,1:T(8,128)(2,1)S(1)}, bf16[128,256]{0,1:T(8,128)(2,1)S(1)}, u32[]{:S(2)}, u32[]{:S(2)}) %collective-permute-start.4) | collective-permute-done | bytes 65568 | tf_op jit(solution)/shard_map/ppermute | solution.py:71
  114.9 2.1 convolution_convert_fusion.1
  117.0 4.8 %collective-permute-done.5 = bf16[128,256]{0,1:T(8,128)(2,1)S(1)} collective-permute-done((bf16[128,256]{0,1:T(8,128)(2,1)S(1)}, bf16[128,256]{0,1:T(8,128)(2,1)S(1)}, u32[]{:S(2)}, u32[]{:S(2)}) %collective-permute-start.5) | collective-permute-done | bytes 65568 | tf_op jit(solution)/shard_map/ppermute | solution.py:71
  121.9 34.9 %all_gather.15 = bf16[1024,256]{1,0:T(8,128)(2,1)S(1)} all-gather(bf16[128,256]{1,0:T(8,128)(2,1)S(1)} %convolution_convert_fusion.1), channel_id=1, replica_groups=mesh['groups'=2,'seq'=8,'dec'=2] {'seq'}, dimensions={0}, use_global_device_ids=true | all-gather | bytes 589824 | tf_op jit(solution)/shard_map/all_gather | solution.py:75
  157.2 86.7 %all-gather.6.cloned.1.call-done = bf16[4096,1024]{1,0:T(8,128)(2,1)} async-done(((bf16[512,1024]{1,0:T(8,128)(2,1)}), bf16[4096,1024]{1,0:T(8,128)(2,1)}) %all-gather.6.cloned.1.call-update) | async-done | bytes 8388624 | tf_op jit(solution)/shard_map/all_gather | solution.py:41
  244.0 4.7 %convolution_bitcast_fusion = f32[16,8,8,128]{3,1,2,0:T(8,128)S(1)} fusion(bf16[4096,1024]{1,0:T(8,128)(2,1)} %all-gather.6.cloned.1.call-done, bf16[128,4096]{1,0:T(8,128)(2,1)S(1)} %copy-done.2, f32[4096]{0:T(1024)S(1)} %copy-done.4, f32[128]{0:T(128)S(1)} %add_rsqrt_fusion), kind=kOutput, calls=%fused_computation.24 | convolution fusion | flops 1075838976 | bytes 9978368 | tf_op jit(solution)/shard_map/dot_general | solution.py:38
  249.3 7.8 %conditional.1 = (f32[2,4,128,1]{2,1,0,3:T(4,128)S(1)}, f32[2,4,128,128]{3,2,1,0:T(8,128)S(1)}) conditional(s32[]{:T(128)} %convert_element_type.46, () %tuple.25, (pred[128,1024]{0,1:T(8,128)(4,1)S(1)}, s32[]{:T(128)}, s32[]{:T(128)}, bf16[2048,256]{0,1:T(8,128)(2,1)S(1)}, bf16[2,4,128,128]{3,2,1,0:T(8,128)(2,1)S(1)}, ...), branch_computations={%region_2.4_spmd, %region_3.7_spmd.clone} | conditional | flops 548543488 | bytes 33730764 | solution.py:104
  249.5 2.8 %fusion.2 = (f32[2,4,128]{2,1,0:T(4,128)S(1)}, f32[2,1024,4,128]{3,1,2,0:T(8,128)}) fusion(pred[128,1024]{0,1:T(8,128)(4,1)S(1)} %get-tuple-element.114, bf16[1024,2,128,1]{0,2,3,1:T(8,128)(2,1)S(1)} %bitcast.82, bf16[2,4,128,128]{3,2,1,0:T(8,128)(2,1)S(1)} %get-tuple-element.117), kind=kOutput, calls=%fused_computation.4 | convolution fusion | flops 271580160 | bytes 5115904 | tf_op jit(solution)/shard_map/cond/branch_1_fun/ghtd,sgd->ghts/dot_general | solution.py:82
  252.5 3.7 %fusion.6 = f32[2,4,128,128]{3,2,1,0:T(8,128)S(1)} fusion(f32[2,1024,4,128]{3,1,2,0:T(8,128)} %get-tuple-element.139, f32[2,4,128]{2,1,0:T(4,128)S(1)} %get-tuple-element.137, pred[128,1024]{0,1:T(8,128)(4,1)S(1)} %get-tuple-element.114, bf16[1024,2,128,1]{2,1,0,3:T(2,128)(2,1)S(1)} %bitcast.88, f32[2,4,128]{2,1,0:T(4,128)S(1)} %get-tuple-element.136), kind=kOutput, calls=%fused_computation.7 | convolution fusion | flops 272760832 | bytes 5382144 | tf_op jit(solution)/shard_map/cond/branch_1_fun/ghts,sgd->ghtd/dot_general | solution.py:96
  256.2 0.9 fusion.1
  257.5 0.9 convert_element_type.54
  (67 shorter events, 6.7 us)
Async XLA Ops:
  7.2 65.0 %copy-start = (bf16[64,2,4,128]{3,2,1,0:T(4,128)(2,1)S(1)}, bf16[64,2,4,128]{3,2,1,0:T(4,128)(2,1)}, u32[]{:S(2)}) copy-start(bf16[64,2,4,128]{3,2,1,0:T(4,128)(2,1)} %param.21) | copy-start | bytes 393220
  7.2 65.0 %copy-start.5 = (s32[4]{0:T(128)S(1)}, s32[4]{0:T(128)}, u32[]{:S(2)}) copy-start(s32[4]{0:T(128)} %param.20) | copy-start | bytes 52
  7.2 73.5 %copy-start.3 = (s32[16]{0:T(128)S(1)}, s32[16]{0:T(128)}, u32[]{:S(2)}) copy-start(s32[16]{0:T(128)} %param.19) | copy-start | bytes 196
  7.2 54.8 %all-gather.4.cloned.1.call-start = ((), (), s32[]{:S(2)}) async-start(), calls=%async_computation.1 | async-start | bytes 2359296 | tf_op jit(solution)/shard_map/all_gather | solution.py:42
  7.9 107.0 %all-gather.8.cloned.1.call-start = ((), (), s32[]{:S(2)}) async-start(), calls=%async_computation.3 | async-start | bytes 2359296 | tf_op jit(solution)/shard_map/all_gather | solution.py:43
  8.7 106.2 %copy-start.2 = (bf16[128,4096]{1,0:T(8,128)(2,1)S(1)}, bf16[128,4096]{1,0:T(8,128)(2,1)}, u32[]{:S(2)}) copy-start(bf16[128,4096]{1,0:T(8,128)(2,1)} %param.13) | copy-start | bytes 3145732
  8.7 106.2 %copy-start.4 = (f32[4096]{0:T(1024)S(1)}, f32[4096]{0:T(1024)}, u32[]{:S(2)}) copy-start(f32[4096]{0:T(1024)} %param.14) | copy-start | bytes 49156
  8.7 235.3 %all-gather.6.cloned.1.call-start = ((), (), s32[]{:S(2)}) async-start(), calls=%async_computation.2 | async-start | bytes 9437184 | tf_op jit(solution)/shard_map/all_gather | solution.py:41
  65.2 7.0 %collective-permute-start = (bf16[128,256]{0,1:T(8,128)(2,1)S(1)}, bf16[128,256]{0,1:T(8,128)(2,1)S(1)}, u32[]{:S(2)}, u32[]{:S(2)}) collective-permute-start(bf16[128,256]{0,1:T(8,128)(2,1)S(1)} %bitcast.85), channel_id=1, source_target_pairs={{0,2},{2,4},{4,6},{6,8},{8,10},{10,12},{12,14},{14,0},{1,3},{3,5},... | collective-permute-start | bytes 196616 | tf_op jit(solution)/shard_map/ppermute | solution.py:71
  72.2 8.5 %collective-permute-start.1 = (bf16[128,256]{0,1:T(8,128)(2,1)S(1)}, bf16[128,256]{0,1:T(8,128)(2,1)S(1)}, u32[]{:S(2)}, u32[]{:S(2)}) collective-permute-start(bf16[128,256]{0,1:T(8,128)(2,1)S(1)} %collective-permute-done), channel_id=1, source_target_pairs={{0,2},{2,4},{4,6},{6,8},{8,10},{10,12},{12,14},{14,0},{1,3},{3,5},... | collective-permute-start | bytes 196616 | tf_op jit(solution)/shard_map/ppermute | solution.py:71
  73.2 35.9 %all-to-all-start = ((bf16[64,2,4,128]{3,1,0,2:T(2,128)(2,1)}), bf16[64,2,4,128]{3,1,0,2:T(2,128)(2,1)S(1)}, u32[]{:S(2)}, u32[]{:S(2)}) async-start(bf16[64,2,4,128]{3,1,0,2:T(2,128)(2,1)} %copy.32), calls=%async_computation | async-start | bytes 262144 | tf_op jit(solution)/shard_map/all_to_all | solution.py:120
  80.7 7.0 %collective-permute-start.2 = (bf16[128,256]{0,1:T(8,128)(2,1)S(1)}, bf16[128,256]{0,1:T(8,128)(2,1)S(1)}, u32[]{:S(2)}, u32[]{:S(2)}) collective-permute-start(bf16[128,256]{0,1:T(8,128)(2,1)S(1)} %collective-permute-done.1), channel_id=1, source_target_pairs={{0,2},{2,4},{4,6},{6,8},{8,10},{10,12},{12,14},{14,0},{1,3},{3,5},... | collective-permute-start | bytes 196616 | tf_op jit(solution)/shard_map/ppermute | solution.py:71
  87.6 19.8 %collective-permute-start.3 = (bf16[128,256]{0,1:T(8,128)(2,1)S(1)}, bf16[128,256]{0,1:T(8,128)(2,1)S(1)}, u32[]{:S(2)}, u32[]{:S(2)}) collective-permute-start(bf16[128,256]{0,1:T(8,128)(2,1)S(1)} %collective-permute-done.2), channel_id=1, source_target_pairs={{0,2},{2,4},{4,6},{6,8},{8,10},{10,12},{12,14},{14,0},{1,3},{3,5},... | collective-permute-start | bytes 196616 | tf_op jit(solution)/shard_map/ppermute | solution.py:71
  107.4 7.5 %collective-permute-start.4 = (bf16[128,256]{0,1:T(8,128)(2,1)S(1)}, bf16[128,256]{0,1:T(8,128)(2,1)S(1)}, u32[]{:S(2)}, u32[]{:S(2)}) collective-permute-start(bf16[128,256]{0,1:T(8,128)(2,1)S(1)} %collective-permute-done.3), channel_id=1, source_target_pairs={{0,2},{2,4},{4,6},{6,8},{8,10},{10,12},{12,14},{14,0},{1,3},{3,5},... | collective-permute-start | bytes 196616 | tf_op jit(solution)/shard_map/ppermute | solution.py:71
  114.9 7.0 %collective-permute-start.5 = (bf16[128,256]{0,1:T(8,128)(2,1)S(1)}, bf16[128,256]{0,1:T(8,128)(2,1)S(1)}, u32[]{:S(2)}, u32[]{:S(2)}) collective-permute-start(bf16[128,256]{0,1:T(8,128)(2,1)S(1)} %collective-permute-done.4), channel_id=1, source_target_pairs={{0,2},{2,4},{4,6},{6,8},{8,10},{10,12},{12,14},{14,0},{1,3},{3,5},... | collective-permute-start | bytes 196616 | tf_op jit(solution)/shard_map/ppermute | solution.py:71
  121.9 35.0 %collective-permute-start.6 = (bf16[128,256]{0,1:T(8,128)(2,1)S(1)}, bf16[128,256]{0,1:T(8,128)(2,1)S(1)}, u32[]{:S(2)}, u32[]{:S(2)}) collective-permute-start(bf16[128,256]{0,1:T(8,128)(2,1)S(1)} %collective-permute-done.5), channel_id=1, source_target_pairs={{0,2},{2,4},{4,6},{6,8},{8,10},{10,12},{12,14},{14,0},{1,3},{3,5},... | collective-permute-start | bytes 196616 | tf_op jit(solution)/shard_map/ppermute | solution.py:71
  252.5 3.7 %copy-start.1 = (f32[2,1024,4,128]{3,1,2,0:T(8,128)S(1)}, f32[2,1024,4,128]{3,1,2,0:T(8,128)}, u32[]{:S(2)}) copy-start(f32[2,1024,4,128]{3,1,2,0:T(8,128)} %get-tuple-element.139) | copy-start | bytes 12582916 | tf_op jit(solution)/shard_map/cond
Sparse Core Ops, SparseCore 0:
  10.1 51.8 all-gather.3
  64.2 48.4 all-gather.7
  114.8 129.1 all-gather.5
